TPU v7x, 32 devices: a 4x4x1 block of a 4x4x8 slice. The times are simulated.
32 devices in a mesh: dp: 1 (over z), tp: 32 (over y, x, core).
Axes of the slice: x: 4, y: 4, z: 1, core: 2. Of those that a mesh axis runs over, the one named last changes fastest.
The devices are a block of a 4x4x8 slice.
Arguments:
- hidden: bfloat16 [3, 768, 5120], P('dp')
- grad_out: bfloat16 [3, 768, 5120], P('dp')
- norm_gain: bfloat16 [5120], replicated
- w_query: bfloat16 [5120, 4096], P(None, 'tp')
- w_key: bfloat16 [5120, 1024], replicated
- w_value: bfloat16 [5120, 1024], replicated
- w_out: bfloat16 [4096, 5120], P('tp')
Outputs:
- output 1: bfloat16 [3, 768, 5120], P('dp')
- output 2: bfloat16 [3, 768, 5120], P('dp')
- output 3: float32 [5120], P('dp')
- output 4: float32 [5120, 4096], P('dp', 'tp')
- output 5: float32 [5120, 4096], P('dp', 'tp')
- output 6: float32 [5120, 4096], P('dp', 'tp')
- output 7: float32 [4096, 5120], P(('dp', 'tp'))
All inputs are finite; a program needn't handle non-finite values.
Results may differ from a plain program's by a relative error of at most 0.00989727.
Values sent between devices are 32-bit elements.
A program may use at most 768 MiB of HBM per device.

v0:
```python
import math
import jax
import jax.numpy as jnp
from jax import lax
from jax.sharding import PartitionSpec as P

HEAD_DIM = 128
NORM_EPS = 1.0e-5
ROPE_BASE = 10000.0
MASK_VALUE = -1.0e30
SCORE_SCALE = 1.0 / math.sqrt(HEAD_DIM)


def rope_tables(seq_len):
    positions = jnp.arange(seq_len, dtype=jnp.float32)
    inv_freq = ROPE_BASE ** (-jnp.arange(0, HEAD_DIM, 2, dtype=jnp.float32) / HEAD_DIM)
    angles = positions[:, None] * inv_freq[None, :]
    return jnp.cos(angles), jnp.sin(angles)


def rotate_pairs(tensor, cos_t, sin_t):
    pair_view = tensor.reshape(tensor.shape[:-1] + (HEAD_DIM // 2, 2))
    even_part = pair_view[..., 0]
    odd_part = pair_view[..., 1]
    cos_b = cos_t[:, None, :]
    sin_b = sin_t[:, None, :]
    rotated = jnp.stack([even_part * cos_b - odd_part * sin_b, even_part * sin_b + odd_part * cos_b], axis=-1)
    return rotated.reshape(tensor.shape)


def group_sum(tensor, tp_size, group_size):
    total = tensor
    for level in range(group_size.bit_length() - 1):
        distance = 2 ** level
        partner_pairs = [(source, source ^ distance) for source in range(tp_size)]
        total = total + lax.ppermute(total, 'tp', perm=partner_pairs)
    return total


def solution(mesh):
    tp_size = mesh.shape['tp']

    def block_fn(hidden, grad_out, norm_gain, w_query, w_key, w_value, w_out):
        kv_heads = w_key.shape[1] // HEAD_DIM
        group_size = tp_size // kv_heads
        q_heads_local = w_query.shape[1] // HEAD_DIM
        batch_local, seq_len, d_model = hidden.shape
        kv_index = lax.axis_index('tp') // group_size
        w_kv = jnp.concatenate([
            lax.dynamic_slice_in_dim(w_key, kv_index * HEAD_DIM, HEAD_DIM, axis=1),
            lax.dynamic_slice_in_dim(w_value, kv_index * HEAD_DIM, HEAD_DIM, axis=1)], axis=1)
        cos_t, sin_t = rope_tables(seq_len)

        hidden_f32 = hidden.astype(jnp.float32)
        inv_rms = lax.rsqrt(jnp.mean(hidden_f32 * hidden_f32, axis=-1, keepdims=True) + NORM_EPS)
        unit_rows = hidden_f32 * inv_rms
        gain_f32 = norm_gain.astype(jnp.float32)
        normed = (unit_rows * gain_f32).astype(jnp.bfloat16)
        q_proj = jnp.einsum('bsd,de->bse', normed, w_query, preferred_element_type=jnp.float32)
        q_rot = rotate_pairs(q_proj.reshape(batch_local, seq_len, q_heads_local, HEAD_DIM), cos_t, sin_t).astype(jnp.bfloat16)
        kv_proj = jnp.einsum('bsd,de->bse', normed, w_kv, preferred_element_type=jnp.float32)
        k_rot = rotate_pairs(kv_proj[:, :, None, :HEAD_DIM], cos_t, sin_t)[:, :, 0, :].astype(jnp.bfloat16)
        v_head = kv_proj[:, :, HEAD_DIM:].astype(jnp.bfloat16)
        scores = jnp.einsum('bqjh,bkh->bjqk', q_rot, k_rot, preferred_element_type=jnp.float32) * SCORE_SCALE
        causal = jnp.arange(seq_len)[:, None] >= jnp.arange(seq_len)[None, :]
        attn_probs = jax.nn.softmax(jnp.where(causal, scores, MASK_VALUE), axis=-1)
        probs_bf16 = attn_probs.astype(jnp.bfloat16)
        attn_heads = jnp.einsum('bjqk,bkh->bqjh', probs_bf16, v_head, preferred_element_type=jnp.float32).astype(jnp.bfloat16)
        attn_flat = attn_heads.reshape(batch_local, seq_len, q_heads_local * HEAD_DIM)
        out_part = jnp.einsum('bse,ed->bsd', attn_flat, w_out, preferred_element_type=jnp.float32)
        attn_sum = lax.psum(out_part, 'tp')
        block_out = (hidden_f32 + attn_sum).astype(jnp.bfloat16)

        grad_w_out = jnp.einsum('bse,bsd->ed', attn_flat, grad_out, preferred_element_type=jnp.float32)
        grad_heads = jnp.einsum('bsd,ed->bse', grad_out, w_out, preferred_element_type=jnp.float32).astype(jnp.bfloat16).reshape(batch_local, seq_len, q_heads_local, HEAD_DIM)
        grad_probs = jnp.einsum('bqjh,bkh->bjqk', grad_heads, v_head, preferred_element_type=jnp.float32)
        grad_v = jnp.einsum('bjqk,bqjh->bkh', probs_bf16, grad_heads, preferred_element_type=jnp.float32)
        row_dot = jnp.sum(attn_probs * grad_probs, axis=-1, keepdims=True)
        grad_scores = (attn_probs * (grad_probs - row_dot) * SCORE_SCALE).astype(jnp.bfloat16)
        grad_q_rot = jnp.einsum('bjqk,bkh->bqjh', grad_scores, k_rot, preferred_element_type=jnp.float32)
        grad_k_rot = jnp.einsum('bjqk,bqjh->bkh', grad_scores, q_rot, preferred_element_type=jnp.float32)
        grad_q = rotate_pairs(grad_q_rot, cos_t, -sin_t).astype(jnp.bfloat16).reshape(batch_local, seq_len, q_heads_local * HEAD_DIM)
        grad_k = rotate_pairs(grad_k_rot[:, :, None, :], cos_t, -sin_t)[:, :, 0, :]
        grad_kv = jnp.concatenate([grad_k, grad_v], axis=-1).astype(jnp.bfloat16)
        grad_w_query = jnp.einsum('bsd,bse->de', normed, grad_q, preferred_element_type=jnp.float32)
        grad_w_kv_part = jnp.einsum('bsd,bse->de', normed, grad_kv, preferred_element_type=jnp.float32)
        grad_normed_part = (jnp.einsum('bse,de->bsd', grad_q, w_query, preferred_element_type=jnp.float32)
                            + jnp.einsum('bse,de->bsd', grad_kv, w_kv, preferred_element_type=jnp.float32))
        grad_normed = lax.psum(grad_normed_part, 'tp')
        gain_grad_rows = grad_normed * gain_f32
        grad_hidden = (grad_out.astype(jnp.float32) + inv_rms * (gain_grad_rows - unit_rows * jnp.mean(gain_grad_rows * unit_rows, axis=-1, keepdims=True))).astype(jnp.bfloat16)
        grad_gain = jnp.sum(grad_normed * unit_rows, axis=(0, 1))
        grad_w_kv = group_sum(grad_w_kv_part, tp_size, group_size)
        return block_out, grad_hidden, grad_gain, grad_w_query, grad_w_kv[:, :HEAD_DIM], grad_w_kv[:, HEAD_DIM:], grad_w_out

    act_spec = P('dp', None, None)
    return jax.shard_map(
        block_fn, mesh=mesh,
        in_specs=(act_spec, act_spec, P(None), P(None, 'tp'), P(None, None), P(None, None), P('tp', None)),
        out_specs=(act_spec, act_spec, P('dp'), P('dp', 'tp'), P('dp', 'tp'), P('dp', 'tp'), P(('dp', 'tp'), None)),
        check_vma=False)
```

profile of v0, /device:TPU:97, one launch (start us, length us, event | category | flops | bytes accessed | tf_op | source)
XLA Modules:
  0.0 998.5 jit_solution(10013673119134184497)
XLA Ops:
  8.3 9.9 fusion.11
  18.3 3.0 constant_dynamic-slice_fusion
  25.1 13.0 %fusion.20 = f32[3,768,128]{1,2,0:T(8,128)} fusion(bf16[3,768,5120]{2,1,0:T(8,128)(2,1)} %param.7, f32[5120]{0:T(1024)S(1)} %convert_element_type.58, f32[3,768]{1,0:T(4,128)S(1)} %add_rsqrt_fusion, bf16[5120,128]{1,0:T(8,128)(2,1)} %param.10), kind=kOutput, calls=%fused_computation.27 | convolution fusion | flops 3067084800 | bytes 26113024 | tf_op jit(solution)/shard_map/bsd,de->bse/dot_general | solution.py:59
  38.1 2.9 reshape_reshape.3
  42.5 11.8 %fusion.22 = f32[3,768,256]{1,2,0:T(8,128)S(1)} fusion(bf16[3,768,5120]{2,1,0:T(8,128)(2,1)} %param.7, f32[5120]{0:T(1024)S(1)} %convert_element_type.58, f32[3,768]{1,0:T(4,128)S(1)} %add_rsqrt_fusion, bf16[5120,128]{0,1:T(8,128)(2,1)S(1)} %copy-done.8, bf16[5120,128]{0,1:T(8,128)(2,1)} %copy.72), kind=kOutput, calls=%fused_computation.28 | convolution fusion | flops 6092226560 | bytes 28603392 | tf_op jit(solution)/shard_map/bsd,de->bse/dot_general | solution.py:61
  58.8 16.3 %subtract_convert_fusion.2 = (bf16[3,768,1,64,1]{1,4,3,0,2:T(2,128)(2,1)}, bf16[3,768,1,64,1]{1,4,3,0,2:T(2,128)(2,1)}, bf16[3,768,1,64,1]{1,4,3,0,2:T(2,128)(2,1)S(1)}, bf16[3,768,1,64,1]{1,4,3,0,2:T(2,128)(2,1)S(1)}) fusion(f32[3,768,1,64,2]{1,4,3,0,2:T(2,128)} %reshape_reshape.3, f32[768,64]{0,1:T(8,128)} %get-tuple-element.28, ...), kind=kLoop, calls=%fused_computation.64 | loop fusion | flops 2359296 | bytes 3932160 | tf_op jit(solution)/shard_map/convert.7
  76.6 3.6 pad_maximum_fusion.4
  83.9 2.9 copy-done.2
  88.5 6.8 fusion.48
  97.1 7.1 convolution_convert_fusion
  104.2 6.9 fusion.13
  116.6 3.4 fusion.39
  120.0 18.1 %fusion.43 = f32[3,768,5120]{2,1,0:T(8,128)} fusion(bf16[3,768,128]{1,2,0:T(8,128)(2,1)S(1)} %copy-done.11, bf16[128,5120]{1,0:T(8,128)(2,1)S(1)} %copy-done), kind=kOutput, calls=%fused_computation.47 | convolution fusion | flops 3019898880 | bytes 49086464 | tf_op jit(solution)/shard_map/bse,ed->bsd/dot_general | solution.py:70
  141.9 5.2 subtract_convert_fusion
  149.5 19.6 %fusion.45 = f32[3,768,5120]{2,1,0:T(8,128)} fusion(bf16[3,768,128]{1,2,0:T(8,128)(2,1)} %convert_element_type.70, bf16[5120,128]{1,0:T(8,128)(2,1)} %param.10), kind=kOutput, calls=%fused_computation.49 | convolution fusion | flops 3019898880 | bytes 49086464 | tf_op jit(solution)/shard_map/bse,de->bsd/dot_general | solution.py:87
  173.2 30.1 %convolution_add_fusion = f32[3,768,5120]{2,1,0:T(8,128)} fusion(f32[3,768,5120]{2,1,0:T(8,128)} %fusion.45, bf16[5120,128]{0,1:T(8,128)(2,1)S(1)} %copy-done.9, bf16[5120,128]{0,1:T(8,128)(2,1)S(1)} %copy-done.10, bf16[3,768,128]{1,2,0:T(8,128)(2,1)} %fusion.39, bf16[3,768,128]{1,2,0:T(8,128)(2,1)S(1)} %squeeze_reshape.5), kind=kOutput, calls=%fused_computation.16 | convolution fusion | flops 6059196416 | bytes 98172928 | tf_op jit(solution)/shard_map/bse,de->bsd/dot_general | solution.py:88
  204.4 14.2 %convolution_bitcast_fusion = f32[5120,256]{1,0:T(8,128)S(1)} fusion(bf16[3,768,5120]{2,1,0:T(8,128)(2,1)} %param.7, f32[5120]{0:T(1024)S(1)} %convert_element_type.58, f32[3,768]{1,0:T(4,128)S(1)} %add_rsqrt_fusion, bf16[3,768,128]{1,2,0:T(8,128)(2,1)S(1)} %copy-done.15, bf16[3,768,128]{1,2,0:T(8,128)(2,1)S(1)} %squeeze_reshape.5), kind=kOutput, calls=%fused_computation.25 | convolution fusion | flops 6089342976 | bytes 30045184 | tf_op jit(solution)/shard_map/bsd,bse->de/dot_general | solution.py:86
  220.7 10.6 %collective-permute-done = f32[5120,256]{1,0:T(8,128)S(1)} collective-permute-done((f32[5120,256]{1,0:T(8,128)S(1)}, f32[5120,256]{1,0:T(8,128)S(1)}, u32[]{:S(2)}, u32[]{:S(2)}) %collective-permute-start) | collective-permute-done | bytes 5242912 | tf_op jit(solution)/shard_map/ppermute | solution.py:36
  233.1 12.4 %convolution_bitcast_fusion.1 = f32[128,5120]{1,0:T(8,128)} fusion(bf16[3,768,128]{1,2,0:T(8,128)(2,1)S(1)} %copy-done.12, bf16[3,768,5120]{2,1,0:T(8,128)(2,1)} %param.8), kind=kOutput, calls=%fused_computation.31 | convolution fusion | flops 3019898880 | bytes 26804224 | tf_op jit(solution)/shard_map/bse,bsd->ed/dot_general | solution.py:74
  245.5 14.0 %fusion.26 = f32[5120,128]{1,0:T(8,128)} fusion(bf16[3,768,128]{1,2,0:T(8,128)(2,1)S(1)} %copy-done.14, bf16[3,768,5120]{2,1,0:T(8,128)(2,1)} %param.7, f32[5120]{0:T(1024)S(1)} %convert_element_type.58, f32[3,768]{1,0:T(4,128)S(1)} %add_rsqrt_fusion), kind=kOutput, calls=%fused_computation.32 | convolution fusion | flops 3067084800 | bytes 26833920 | tf_op jit(solution)/shard_map/bsd,bse->de/dot_general | solution.py:85
  259.5 143.4 %collective-permute-done.1 = f32[5120,256]{1,0:T(8,128)S(1)} collective-permute-done((f32[5120,256]{1,0:T(8,128)S(1)}, f32[5120,256]{1,0:T(8,128)S(1)}, u32[]{:S(2)}, u32[]{:S(2)}) %collective-permute-start.1) | collective-permute-done | bytes 5242912 | tf_op jit(solution)/shard_map/ppermute | solution.py:36
  406.3 497.7 %all-reduce.3.cloned.1.call-done = (f32[3,768,5120]{2,1,0:T(8,128)}, f32[3,768,5120]{2,1,0:T(8,128)}) async-done(((f32[3,768,5120]{2,1,0:T(8,128)}, f32[3,768,5120]{2,1,0:T(8,128)}), (f32[3,768,5120]{2,1,0:T(8,128)}, f32[3,768,5120]{2,1,0:T(8,128)})) %all-reduce.3.cloned.1.call-update) | async-done | bytes 94371856 | tf_op jit(solution)/shard_map/psum | solution.py:71
  904.0 26.4 %fusion.10 = (f32[5120]{0:T(1024)}, f32[3,768]{1,0:T(4,128)S(1)}) fusion(f32[3,768,5120]{2,1,0:T(8,128)} %get-tuple-element.10, bf16[3,768,5120]{2,1,0:T(8,128)(2,1)} %param.7, f32[3,768]{1,0:T(4,128)S(1)} %add_rsqrt_fusion, f32[5120]{0:T(1024)S(1)} %convert_element_type.58), kind=kLoop, calls=%fused_computation.13 | loop fusion | flops 82567936 | bytes 70838272 | tf_op jit(solution)/shard_map/reduce_sum | solution.py:92
  930.4 60.7 %fusion.9 = (bf16[3,768,5120]{2,1,0:T(8,128)(2,1)}, bf16[3,768,5120]{2,1,0:T(8,128)(2,1)}) fusion(bf16[3,768,5120]{2,1,0:T(8,128)(2,1)} %param.7, bf16[3,768,5120]{2,1,0:T(8,128)(2,1)} %param.8, f32[3,768,5120]{2,1,0:T(8,128)} %get-tuple-element.10, f32[3,768]{1,0:T(4,128)S(1)} %broadcast_multiply_fusion, f32[5120]{0:T(1024)S(1)} %convert_element_type.58, ...), kind=kLoop, calls=%fused_computation.12 | loop fusion | flops 129761280 | bytes 188782592 | tf_op jit(solution)/shard_map/convert_element_type | solution.py:91
  (81 shorter events, 43.5 us)
Async XLA Ops:
  7.2 88.1 %copy-start = (bf16[128,5120]{1,0:T(8,128)(2,1)S(1)}, bf16[128,5120]{1,0:T(8,128)(2,1)}, u32[]{:S(2)}) copy-start(bf16[128,5120]{1,0:T(8,128)(2,1)} %param.13) | copy-start | bytes 3932164
  7.2 896.8 %all-reduce.3.cloned.1.call-start = ((), (), s32[]{:S(2)}) async-start(), calls=%async_computation | async-start | bytes 188743680 | tf_op jit(solution)/shard_map/psum | solution.py:71
  25.1 17.4 %copy-start.8 = (bf16[5120,128]{0,1:T(8,128)(2,1)S(1)}, bf16[5120,128]{0,1:T(8,128)(2,1)}, u32[]{:S(2)}) copy-start(bf16[5120,128]{0,1:T(8,128)(2,1)} %copy.73) | copy-start | bytes 3932164
  76.6 7.3 copy-start.4
  82.2 6.2 copy-start.17
  83.9 3.0 copy-start.2
  86.8 8.5 slice-start
  86.8 8.5 slice-start.1
  88.4 6.9 slice-start.2
  88.4 6.9 slice-start.3
  88.4 7.9 slice-start.4
  88.4 8.6 slice-start.5
  104.2 6.9 copy-start.3
  111.1 4.9 copy-start.5
  113.6 3.0 copy-start.18
  116.6 3.4 copy-start.11
  149.5 19.6 %copy-start.13 = (bf16[3,768,1,64,1]{1,4,3,0,2:T(2,128)(2,1)S(1)}, bf16[3,768,1,64,1]{1,4,3,0,2:T(2,128)(2,1)}, u32[]{:S(2)}) copy-start(bf16[3,768,1,64,1]{1,4,3,0,2:T(2,128)(2,1)} %get-tuple-element.16) | copy-start | bytes 884740
  149.5 23.7 %copy-start.9 = (bf16[5120,128]{0,1:T(8,128)(2,1)S(1)}, bf16[5120,128]{0,1:T(8,128)(2,1)}, u32[]{:S(2)}) copy-start(bf16[5120,128]{0,1:T(8,128)(2,1)} %copy.73) | copy-start | bytes 3932164
  149.5 23.7 %copy-start.10 = (bf16[5120,128]{0,1:T(8,128)(2,1)S(1)}, bf16[5120,128]{0,1:T(8,128)(2,1)}, u32[]{:S(2)}) copy-start(bf16[5120,128]{0,1:T(8,128)(2,1)} %copy.72) | copy-start | bytes 3932164
  218.6 14.5 %copy-start.12 = (bf16[3,768,128]{1,2,0:T(8,128)(2,1)S(1)}, bf16[3,768,128]{1,2,0:T(8,128)(2,1)}, u32[]{:S(2)}) copy-start(bf16[3,768,128]{1,2,0:T(8,128)(2,1)} %fusion.48) | copy-start | bytes 1769476
  218.6 12.8 %collective-permute-start = (f32[5120,256]{1,0:T(8,128)S(1)}, f32[5120,256]{1,0:T(8,128)S(1)}, u32[]{:S(2)}, u32[]{:S(2)}) collective-permute-start(f32[5120,256]{1,0:T(8,128)S(1)} %convolution_bitcast_fusion), channel_id=1, source_target_pairs={{0,1},{1,0},{2,3},{3,2},{4,5},{5,4},{6,7},{7,6},{8,9},{9,8},{10,11... | collective-permute-start | bytes 15728648 | tf_op jit(solution)/shard_map/ppermute | solution.py:36
  232.0 13.5 %copy-start.14 = (bf16[3,768,128]{1,2,0:T(8,128)(2,1)S(1)}, bf16[3,768,128]{1,2,0:T(8,128)(2,1)}, u32[]{:S(2)}) copy-start(bf16[3,768,128]{1,2,0:T(8,128)(2,1)} %convert_element_type.70) | copy-start | bytes 1769476
  232.0 170.9 %collective-permute-start.1 = (f32[5120,256]{1,0:T(8,128)S(1)}, f32[5120,256]{1,0:T(8,128)S(1)}, u32[]{:S(2)}, u32[]{:S(2)}) collective-permute-start(f32[5120,256]{1,0:T(8,128)S(1)} %add.69), channel_id=1, source_target_pairs={{0,2},{1,3},{2,0},{3,1},{4,6},{5,7},{6,4},{7,5},{8,10},{9,11},{10,... | collective-permute-start | bytes 15728648 | tf_op jit(solution)/shard_map/ppermute | solution.py:36
  930.4 60.7 %copy-start.1 = (bf16[128,5120]{1,0:T(8,128)(2,1)S(1)}, bf16[128,5120]{1,0:T(8,128)(2,1)}, u32[]{:S(2)}) copy-start(bf16[128,5120]{1,0:T(8,128)(2,1)} %param.13) | copy-start | bytes 3932164
  (4 other events, 6.7 us)
Sparse Core Ops, SparseCore 0:
  203.5 700.4 all-reduce.2
where the time goes:
time: 1000 us; the launch traced here: 998 us
  waiting for transfers between devices  652 us (65%)
  matrix products  162 us (16%)
  other arithmetic  135 us (14%)
  local copies, waits for them, and re-layouts  31.6 us (3%)
  between operations  14.9 us (1%)
    psum x1, waiting for transfers between devices, block_fn(): attn_sum = lax.psum(out_part, 'tp')  498 us
    ppermute x2, waiting for transfers between devices, group_sum(): total = total + lax.ppermute(total, 'tp', perm=partner_pairs)  154 us
    convert_element_type x1, other arithmetic, block_fn(): (grad_out.astype(jnp.float32) + inv_rms * (gain_grad_rows - unit_rows * j...  60.7 us
    dot_general x1, matrix products, block_fn(): jnp.einsum('bse,de->bsd', grad_kv, w_kv, preferred_element_type=jnp.float32)  30.1 us
    reduce_sum x1, other arithmetic, block_fn(): grad_gain = jnp.sum(grad_normed * unit_rows, axis=(0, 1))  26.4 us
    another operation x3, other arithmetic  24 us
  transfers between devices with their start and end apart: 3, of which 3 were waited for; matrix products, arithmetic and copies ran while one was open for 4% of the time, Pallas kernels for 0%

commit v1 on v0

--- a/solution.py
+++ b/solution.py
@@ -68,7 +68,8 @@
         attn_heads = jnp.einsum('bjqk,bkh->bqjh', probs_bf16, v_head, preferred_element_type=jnp.float32).astype(jnp.bfloat16)
         attn_flat = attn_heads.reshape(batch_local, seq_len, q_heads_local * HEAD_DIM)
         out_part = jnp.einsum('bse,ed->bsd', attn_flat, w_out, preferred_element_type=jnp.float32)
-        attn_sum = lax.psum(out_part, 'tp')
+        attn_rows = lax.psum_scatter(out_part.reshape(batch_local * seq_len, d_model), 'tp', scatter_dimension=0, tiled=True)
+        attn_sum = lax.all_gather(attn_rows, 'tp', axis=0, tiled=True).reshape(batch_local, seq_len, d_model)
         block_out = (hidden_f32 + attn_sum).astype(jnp.bfloat16)
 
         grad_w_out = jnp.einsum('bse,bsd->ed', attn_flat, grad_out, preferred_element_type=jnp.float32)
@@ -81,16 +82,23 @@
         grad_k_rot = jnp.einsum('bjqk,bqjh->bkh', grad_scores, q_rot, preferred_element_type=jnp.float32)
         grad_q = rotate_pairs(grad_q_rot, cos_t, -sin_t).astype(jnp.bfloat16).reshape(batch_local, seq_len, q_heads_local * HEAD_DIM)
         grad_k = rotate_pairs(grad_k_rot[:, :, None, :], cos_t, -sin_t)[:, :, 0, :]
-        grad_kv = jnp.concatenate([grad_k, grad_v], axis=-1).astype(jnp.bfloat16)
-        grad_w_query = jnp.einsum('bsd,bse->de', normed, grad_q, preferred_element_type=jnp.float32)
-        grad_w_kv_part = jnp.einsum('bsd,bse->de', normed, grad_kv, preferred_element_type=jnp.float32)
+        grad_kv_f32 = jnp.concatenate([grad_k, grad_v], axis=-1)
+        grad_kv = grad_kv_f32.astype(jnp.bfloat16)
         grad_normed_part = (jnp.einsum('bse,de->bsd', grad_q, w_query, preferred_element_type=jnp.float32)
                             + jnp.einsum('bse,de->bsd', grad_kv, w_kv, preferred_element_type=jnp.float32))
-        grad_normed = lax.psum(grad_normed_part, 'tp')
-        gain_grad_rows = grad_normed * gain_f32
-        grad_hidden = (grad_out.astype(jnp.float32) + inv_rms * (gain_grad_rows - unit_rows * jnp.mean(gain_grad_rows * unit_rows, axis=-1, keepdims=True))).astype(jnp.bfloat16)
-        grad_gain = jnp.sum(grad_normed * unit_rows, axis=(0, 1))
-        grad_w_kv = group_sum(grad_w_kv_part, tp_size, group_size)
+        rows = batch_local * seq_len // tp_size
+        grad_rows = lax.psum_scatter(grad_normed_part.reshape(batch_local * seq_len, d_model), 'tp', scatter_dimension=0, tiled=True)
+        first = lax.axis_index('tp') * rows
+        unit_own = lax.dynamic_slice_in_dim(unit_rows.reshape(batch_local * seq_len, d_model), first, rows, axis=0)
+        inv_own = lax.dynamic_slice_in_dim(inv_rms.reshape(batch_local * seq_len, 1), first, rows, axis=0)
+        gain_own = grad_rows * gain_f32
+        delta = inv_own * (gain_own - unit_own * jnp.mean(gain_own * unit_own, axis=-1, keepdims=True))
+        grad_gain = lax.psum(jnp.sum(grad_rows * unit_own, axis=0), 'tp')
+        delta_all = lax.all_gather(delta, 'tp', axis=0, tiled=True).reshape(batch_local, seq_len, d_model)
+        grad_hidden = (grad_out.astype(jnp.float32) + delta_all).astype(jnp.bfloat16)
+        grad_kv_sum = group_sum(grad_kv_f32, tp_size, group_size).astype(jnp.bfloat16)
+        grad_w_query = jnp.einsum('bsd,bse->de', normed, grad_q, preferred_element_type=jnp.float32)
+        grad_w_kv = jnp.einsum('bsd,bse->de', normed, grad_kv_sum, preferred_element_type=jnp.float32)
         return block_out, grad_hidden, grad_gain, grad_w_query, grad_w_kv[:, :HEAD_DIM], grad_w_kv[:, HEAD_DIM:], grad_w_out
 
     act_spec = P('dp', None, None)

time: 1000 us -> 886 us (0.89)
  waiting for transfers between devices: 652 us -> 491 us
  blocking collectives: 0 us -> 49.3 us
  other arithmetic: 135 us -> 119 us
    psum x1 -> x0, waiting for transfers between devices: 498 us -> none  [block_fn(): attn_sum = lax.psum(out_part, 'tp')]
    reduce_scatter x0 -> x2, waiting for transfers between devices: none -> 358 us  [the longest x1 203 us: block_fn(): lax.psum_scatter(out_part.reshape(batch_local * seq_len, d_model), 'tp',...]
    ppermute x2, waiting for transfers between devices: 154 us -> 66.7 us  [group_sum(): total = total + lax.ppermute(total, 'tp', perm=partner_pairs)]
    all_gather x0 -> x2, waiting for transfers between devices: none -> 66.3 us  [the longest x1 49.4 us: block_fn(): lax.all_gather(attn_rows, 'tp', axis=0, tiled=True)]
    mul x0 -> x2, other arithmetic: none -> 49.9 us  [the longest x1 47.1 us: block_fn(): unit_rows = hidden_f32 * inv_rms]
    psum x0 -> x1, blocking collectives: none -> 49.3 us  [block_fn(): grad_gain = lax.psum(jnp.sum(grad_rows * unit_own, axis=0), 'tp')]
    convert_element_type x1, other arithmetic: 60.7 us -> 30.3 us  [block_fn(): (grad_out.astype(jnp.float32) + delta_all).astype(jnp.bfloat16)]
    reduce_sum x1, other arithmetic: 26.4 us -> 2.31 us  [block_fn(): grad_gain = lax.psum(jnp.sum(grad_rows * unit_own, axis=0), 'tp')]
  transfers between devices with their start and end apart: 3 -> 6, of which waited for: 3 -> 6; matrix products, arithmetic and copies ran while one was open for 4% -> 21% of each run, Pallas kernels for 0% -> 0%
where the time goes in v1:
time: 886 us; the launch traced here: 877 us
  waiting for transfers between devices  491 us (55%)
  matrix products  167 us (19%)
  other arithmetic  119 us (13%)
  blocking collectives  49.3 us (6%)
  local copies, waits for them, and re-layouts  32.9 us (4%)
  between operations  14.6 us (2%)
    reduce_scatter x1, waiting for transfers between devices, block_fn(): lax.psum_scatter(out_part.reshape(batch_local * seq_len, d_model), 'tp',...  203 us
    reduce_scatter x1, waiting for transfers between devices, block_fn(): lax.psum_scatter(grad_normed_part.reshape(batch_local * seq_len, d_model)...  155 us
    ppermute x2, waiting for transfers between devices, group_sum(): total = total + lax.ppermute(total, 'tp', perm=partner_pairs)  66.7 us
    all_gather x1, waiting for transfers between devices, block_fn(): lax.all_gather(attn_rows, 'tp', axis=0, tiled=True)  49.4 us
    psum x1, blocking collectives, block_fn(): grad_gain = lax.psum(jnp.sum(grad_rows * unit_own, axis=0), 'tp')  49.3 us
    mul x1, other arithmetic, block_fn(): unit_rows = hidden_f32 * inv_rms  47.1 us
    dot_general x1, matrix products, block_fn(): jnp.einsum('bse,de->bsd', grad_kv, w_kv, preferred_element_type=jnp.float32)  30.9 us
    convert_element_type x1, other arithmetic, block_fn(): (grad_out.astype(jnp.float32) + delta_all).astype(jnp.bfloat16)  30.3 us
  transfers between devices with their start and end apart: 6, of which 6 were waited for; matrix products, arithmetic and copies ran while one was open for 21% of the time, Pallas kernels for 0%

profile of v1, /device:TPU:97, one launch (start us, length us, event | category | flops | bytes accessed | tf_op | source)
XLA Modules:
  0.0 876.7 jit_solution(10154412187215129649)
XLA Ops:
  15.8 10.4 %fusion = f32[3,768]{1,0:T(4,128)S(1)} fusion(bf16[3,768,5120]{2,1,0:T(8,128)(2,1)} %param.7), kind=kLoop, calls=%fused_computation.3 | loop fusion | flops 35387136 | bytes 23602176 | tf_op jit(solution)/shard_map/reduce_sum | solution.py:55
  26.8 11.6 %fusion.8 = f32[3,768,256]{1,2,0:T(8,128)S(1)} fusion(f32[5120]{0:T(1024)S(1)} %convert_element_type.63, f32[3,768]{1,0:T(4,128)S(1)} %get-tuple-element.26, bf16[3,768,5120]{2,1,0:T(8,128)(2,1)} %param.7, bf16[5120,128]{0,1:T(8,128)(2,1)S(1)} %copy-done.6, bf16[5120,128]{0,1:T(8,128)(2,1)S(1)} %copy-done.5), kind=kOutput, calls=%fused_computation.19 | convolution fusion | flops 6092226560 | bytes 28603392 | tf_op jit(solution)/shard_map/bsd,de->bse/dot_general | solution.py:61
  43.0 13.0 %fusion.7 = f32[3,768,128]{1,2,0:T(8,128)} fusion(f32[5120]{0:T(1024)S(1)} %convert_element_type.63, f32[3,768]{1,0:T(4,128)S(1)} %get-tuple-element.26, bf16[3,768,5120]{2,1,0:T(8,128)(2,1)} %param.7, bf16[5120,128]{1,0:T(8,128)(2,1)} %param.10), kind=kOutput, calls=%fused_computation.18 | convolution fusion | flops 3067084800 | bytes 26113024 | tf_op jit(solution)/shard_map/bsd,de->bse/dot_general | solution.py:59
  59.6 5.4 subtract_convert_fusion.1
  82.4 19.2 %fusion.40 = f32[2304,5120]{1,0:T(8,128)} fusion(bf16[2304,128]{1,0:T(8,128)(2,1)} %bitcast.127, bf16[128,5120]{1,0:T(8,128)(2,1)S(1)} %copy-done), kind=kOutput, calls=%fused_computation.77 | convolution fusion | flops 3019898880 | bytes 49086464 | tf_op jit(solution)/shard_map/bse,ed->bsd/dot_general | solution.py:70
  102.1 202.9 %reduce-scatter.3.cloned.1.call-done = f32[72,5120]{1,0:T(8,128)} async-done(((f32[2304,5120]{1,0:T(8,128)}), f32[72,5120]{1,0:T(8,128)}) %reduce-scatter.3.cloned.1.call-update) | async-done | bytes 1474576 | tf_op jit(solution)/shard_map/reduce_scatter | solution.py:71
  305.2 11.2 %convolution_convert_fusion = bf16[3,768,128]{2,1,0:T(8,128)(2,1)S(1)} fusion(bf16[3,768,5120]{2,1,0:T(8,128)(2,1)} %param.8, bf16[128,5120]{1,0:T(8,128)(2,1)S(1)} %copy-done), kind=kOutput, calls=%fused_computation.40 | convolution fusion | flops 3020193792 | bytes 25493504 | tf_op jit(solution)/shard_map/bsd,ed->bse/dot_general | solution.py:76
  316.4 5.2 fusion.2
  321.6 4.6 fusion.13
  331.7 4.3 fusion.41
  347.3 4.8 fusion.14
  352.2 18.2 %fusion.23 = f32[3,768,5120]{2,1,0:T(8,128)} fusion(bf16[3,768,128]{1,2,0:T(8,128)(2,1)S(1)} %copy-done.9, bf16[5120,128]{1,0:T(8,128)(2,1)S(1)} %copy-done.11), kind=kOutput, calls=%fused_computation.42 | convolution fusion | flops 3019898880 | bytes 49086464 | tf_op jit(solution)/shard_map/bse,de->bsd/dot_general | solution.py:87
  370.4 30.9 %convolution_add_fusion = f32[3,768,5120]{2,1,0:T(8,128)} fusion(f32[3,768,5120]{2,1,0:T(8,128)} %fusion.23, bf16[5120,128]{0,1:T(8,128)(2,1)} %copy.71, bf16[5120,128]{0,1:T(8,128)(2,1)} %copy.70, f32[3,768,128]{1,2,0:T(8,128)S(1)} %fusion.14, f32[3,768,128]{1,2,0:T(8,128)S(1)} %squeeze_reshape.4), kind=kOutput, calls=%fused_computation.7 | convolution fusion | flops 6059196416 | bytes 99352576 | tf_op jit(solution)/shard_map/bse,de->bsd/dot_general | solution.py:88
  402.1 49.4 %all-gather.3.cloned.1.call-done = f32[2304,5120]{1,0:T(8,128)} async-done(((f32[72,5120]{1,0:T(8,128)}), f32[2304,5120]{1,0:T(8,128)}) %all-gather.3.cloned.1.call-update) | async-done | bytes 47185936 | tf_op jit(solution)/shard_map/all_gather | solution.py:72
  451.4 47.1 %convert_multiply_fusion = (f32[3,768,5120]{2,1,0:T(8,128)}, bf16[3,768,5120]{2,1,0:T(8,128)(2,1)}) fusion(bf16[3,768,5120]{2,1,0:T(8,128)(2,1)} %param.7, f32[3,768]{1,0:T(4,128)S(1)} %get-tuple-element.26, f32[3,768,5120]{2,1,0:T(8,128)} %bitcast.125), kind=kLoop, calls=%fused_computation.1 | loop fusion | flops 47185920 | bytes 141566976 | tf_op jit(solution)/shard_map/mul | solution.py:56
  498.6 154.8 %reduce-scatter.5.cloned.1.call-done = f32[72,5120]{1,0:T(8,128)} async-done(((f32[2304,5120]{1,0:T(8,128)}), f32[72,5120]{1,0:T(8,128)}) %reduce-scatter.5.cloned.1.call-update) | async-done | bytes 1474576 | tf_op jit(solution)/shard_map/reduce_scatter | solution.py:90
  659.7 4.2 collective-permute-done
  665.5 12.6 %convolution_bitcast_fusion.1 = f32[128,5120]{1,0:T(8,128)} fusion(bf16[3,768,5120]{2,1,0:T(8,128)(2,1)} %param.8, bf16[3,128,768]{2,1,0:T(8,128)(2,1)S(1)} %copy-done.7), kind=kOutput, calls=%fused_computation.22 | convolution fusion | flops 3019898880 | bytes 26804224 | tf_op jit(solution)/shard_map/bse,bsd->ed/dot_general | solution.py:75
  678.1 13.8 %fusion.11 = f32[5120,128]{1,0:T(8,128)} fusion(bf16[3,768,128]{1,2,0:T(8,128)(2,1)S(1)} %copy-done.10, f32[5120]{0:T(1024)S(1)} %copy-done.16, f32[3,768]{1,0:T(4,128)S(1)} %get-tuple-element.26, bf16[3,768,5120]{2,1,0:T(8,128)(2,1)} %param.7), kind=kOutput, calls=%fused_computation.23 | convolution fusion | flops 3067084800 | bytes 26833920 | tf_op jit(solution)/shard_map/bsd,bse->de/dot_general | solution.py:100
  691.9 62.5 %collective-permute-done.1 = f32[3,768,256]{1,2,0:T(8,128)} collective-permute-done((f32[3,768,256]{1,2,0:T(8,128)S(1)}, f32[3,768,256]{1,2,0:T(8,128)}, u32[]{:S(2)}, u32[]{:S(2)}) %collective-permute-start.1) | collective-permute-done | bytes 2359328 | tf_op jit(solution)/shard_map/ppermute | solution.py:36
  754.5 15.8 %convolution_bitcast_fusion = f32[5120,256]{1,0:T(8,128)S(1)} fusion(f32[5120]{0:T(1024)S(1)} %copy-done.16, f32[3,768]{1,0:T(4,128)S(1)} %get-tuple-element.26, bf16[3,768,5120]{2,1,0:T(8,128)(2,1)} %param.7, f32[3,768,256]{1,2,0:T(8,128)} %copy-done.8, f32[3,768,256]{1,2,0:T(8,128)} %collective-permute-done.1), kind=kOutput, calls=%fused_computation.16 | convolution fusion | flops 6088163328 | bytes 33584128 | tf_op jit(solution)/shard_map/bsd,bse->de/dot_general | solution.py:101
  773.0 49.3 %psum.7 = f32[5120]{0:T(1024)} all-reduce(f32[5120]{0:T(1024)S(1)} %get-tuple-element.7), channel_id=1, replica_groups=mesh['dp'=1,'tp'=32] {'tp'}, use_global_device_ids=true, to_apply=%region_8.9 | all-reduce | flops 5120 | bytes 40960 | tf_op jit(solution)/shard_map/psum | solution.py:96
  822.4 17.0 %all-gather.5.cloned.1.call-done = f32[2304,5120]{1,0:T(8,128)} async-done(((f32[72,5120]{1,0:T(8,128)}), f32[2304,5120]{1,0:T(8,128)}) %all-gather.5.cloned.1.call-update) | async-done | bytes 47185936 | tf_op jit(solution)/shard_map/all_gather | solution.py:97
  839.3 30.3 %add_convert_fusion = bf16[3,768,5120]{2,1,0:T(8,128)(2,1)} fusion(f32[3,768,5120]{2,1,0:T(8,128)} %bitcast.124, bf16[3,768,5120]{2,1,0:T(8,128)(2,1)} %param.8), kind=kLoop, calls=%fused_computation.5 | loop fusion | flops 35389440 | bytes 94371840 | tf_op jit(solution)/shard_map/convert_element_type | solution.py:98
  (85 shorter events, 63.5 us)
Async XLA Ops:
  7.2 75.2 %copy-start = (bf16[128,5120]{1,0:T(8,128)(2,1)S(1)}, bf16[128,5120]{1,0:T(8,128)(2,1)}, u32[]{:S(2)}) copy-start(bf16[128,5120]{1,0:T(8,128)(2,1)} %param.13) | copy-start | bytes 3932164
  7.2 297.8 %reduce-scatter.3.cloned.1.call-start = ((), (), s32[]{:S(2)}) async-start(), calls=%async_computation.2 | async-start | bytes 48660480 | tf_op jit(solution)/shard_map/reduce_scatter | solution.py:71
  15.8 11.0 %copy-start.18 = (bf16[5120]{0:T(1024)(128)(2,1)S(1)}, bf16[5120]{0:T(1024)(128)(2,1)}, u32[]{:S(2)}) copy-start(bf16[5120]{0:T(1024)(128)(2,1)} %param.9) | copy-start | bytes 30724
  15.8 11.0 %copy-start.5 = (bf16[5120,128]{0,1:T(8,128)(2,1)S(1)}, bf16[5120,128]{0,1:T(8,128)(2,1)}, u32[]{:S(2)}) copy-start(bf16[5120,128]{0,1:T(8,128)(2,1)} %copy.70) | copy-start | bytes 3932164
  15.8 11.0 %copy-start.6 = (bf16[5120,128]{0,1:T(8,128)(2,1)S(1)}, bf16[5120,128]{0,1:T(8,128)(2,1)}, u32[]{:S(2)}) copy-start(bf16[5120,128]{0,1:T(8,128)(2,1)} %copy.71) | copy-start | bytes 3932164
  26.8 16.1 %copy-start.15 = (f32[5120]{0:T(1024)}, f32[5120]{0:T(1024)S(1)}, u32[]{:S(2)}) copy-start(f32[5120]{0:T(1024)S(1)} %convert_element_type.63) | copy-start | bytes 61444
  73.6 3.2 copy-start.2
  73.6 3.4 copy-start.13
  101.6 349.8 %all-gather.3.cloned.1.call-start = ((), (), s32[]{:S(2)}) async-start(), calls=%async_computation.3 | async-start | bytes 48660480 | tf_op jit(solution)/shard_map/all_gather | solution.py:72
  305.1 348.2 %reduce-scatter.5.cloned.1.call-start = ((), (), s32[]{:S(2)}) async-start(), calls=%async_computation.4 | async-start | bytes 48660480 | tf_op jit(solution)/shard_map/reduce_scatter | solution.py:90
  305.2 11.2 %copy-start.14 = (f32[3,768,256]{1,2,0:T(8,128)S(1)}, f32[3,768,256]{1,2,0:T(8,128)}, u32[]{:S(2)}) copy-start(f32[3,768,256]{1,2,0:T(8,128)} %copy-done.12) | copy-start | bytes 7077892
  316.4 5.3 copy-start.19
  326.2 1.8 copy-start.3
  347.3 4.8 copy-start.9
  347.3 4.9 copy-start.11
  401.3 438.0 %all-gather.5.cloned.1.call-start = ((), (), s32[]{:S(2)}) async-start(), calls=%async_computation.5 | async-start | bytes 48660480 | tf_op jit(solution)/shard_map/all_gather | solution.py:97
  451.4 201.9 %copy-start.16 = (f32[5120]{0:T(1024)S(1)}, f32[5120]{0:T(1024)}, u32[]{:S(2)}) copy-start(f32[5120]{0:T(1024)} %copy-done.15) | copy-start | bytes 61444
  653.3 2.3 copy-start.4
  658.7 6.8 copy-start.7
  658.7 5.2 collective-permute-start
  664.2 13.9 %copy-start.8 = (f32[3,768,256]{1,2,0:T(8,128)}, f32[3,768,256]{1,2,0:T(8,128)S(1)}, u32[]{:S(2)}) copy-start(f32[3,768,256]{1,2,0:T(8,128)S(1)} %fusion.38) | copy-start | bytes 7077892
  664.2 13.9 %copy-start.10 = (bf16[3,768,128]{1,2,0:T(8,128)(2,1)S(1)}, bf16[3,768,128]{1,2,0:T(8,128)(2,1)}, u32[]{:S(2)}) copy-start(bf16[3,768,128]{1,2,0:T(8,128)(2,1)} %convert_element_type.75) | copy-start | bytes 1769476
  664.2 90.2 %collective-permute-start.1 = (f32[3,768,256]{1,2,0:T(8,128)S(1)}, f32[3,768,256]{1,2,0:T(8,128)}, u32[]{:S(2)}, u32[]{:S(2)}) collective-permute-start(f32[3,768,256]{1,2,0:T(8,128)S(1)} %fusion.38), channel_id=1, source_target_pairs={{0,2},{1,3},{2,0},{3,1},{4,6},{5,7},{6,4},{7,5},{8,10},{9,11},{10,... | collective-permute-start | bytes 7077896 | tf_op jit(solution)/shard_map/ppermute | solution.py:36
  839.3 30.3 %copy-start.1 = (bf16[128,5120]{1,0:T(8,128)(2,1)S(1)}, bf16[128,5120]{1,0:T(8,128)(2,1)}, u32[]{:S(2)}) copy-start(bf16[128,5120]{1,0:T(8,128)(2,1)} %param.13) | copy-start | bytes 3932164
  (2 other events, 2.1 us)
Sparse Core Ops, SparseCore 0:
  101.7 203.2 reduce-scatter.2
  307.1 144.2 all-gather.2
  455.2 198.0 reduce-scatter.4
  658.6 180.6 all-gather.4

commit v2 on v0

v2 whole, which is shorter than its diff:
```python
import functools
import math
import jax
import jax.numpy as jnp
from jax import lax
from jax.experimental import pallas as pl
from jax.experimental.pallas import tpu as pltpu
from jax.sharding import PartitionSpec as P

HEAD_DIM = 128
NORM_EPS = 1.0e-5
ROPE_BASE = 10000.0
MASK_VALUE = -1.0e30
SCORE_SCALE = 1.0 / math.sqrt(HEAD_DIM)
RING = 4
CORES = 2
ROW_DEVICES = RING * CORES
CHUNKS = 6
VMEM_BYTES = 56 * 1024 * 1024


def rope_tables(seq_len):
    positions = jnp.arange(seq_len, dtype=jnp.float32)
    inv_freq = ROPE_BASE ** (-jnp.arange(0, HEAD_DIM, 2, dtype=jnp.float32) / HEAD_DIM)
    angles = positions[:, None] * inv_freq[None, :]
    return jnp.cos(angles), jnp.sin(angles)


def rotate_pairs(tensor, cos_t, sin_t):
    pair_view = tensor.reshape(tensor.shape[:-1] + (HEAD_DIM // 2, 2))
    even_part = pair_view[..., 0]
    odd_part = pair_view[..., 1]
    cos_b = cos_t[:, None, :]
    sin_b = sin_t[:, None, :]
    rotated = jnp.stack([even_part * cos_b - odd_part * sin_b, even_part * sin_b + odd_part * cos_b], axis=-1)
    return rotated.reshape(tensor.shape)


class Place:
    def __init__(self):
        index = lax.axis_index('tp')
        self.c = lax.rem(index, CORES)
        self.x = lax.rem(index // CORES, RING)
        self.y = index // ROW_DEVICES

    def at(self, y, x, c):
        return {'tp': (y * RING + x) * CORES + c}


def turn(position, by):
    return lax.rem(position + (by % RING), RING)


def exchange_kernel(backward, chunks, *refs):
    if backward:
        (act_hbm, kv_hbm, wt_ref, wkv_ref, x_ref, dout_ref, inv_ref, gain_ref, out_ref, kv_out,
         gath, wb, part, ring, kvp, kv_core, kv_send, kv_chip, rowpart, rowall,
         gs_sem, gr_sem, rs_sem, rr_sem, ks_sem, kr_sem, ms_sem, mr_sem, loc_sem) = refs
    else:
        act_hbm, wt_ref, x_ref, out_ref, gath, wb, part, ring, gs_sem, gr_sem, rs_sem, rr_sem, loc_sem = refs
    me = Place()
    x, y, c = me.x, me.y, me.c
    xr, xl, xo = turn(x, 1), turn(x, -1), turn(x, 2)
    yu, yd = turn(y, 1), turn(y, -1)
    other = 1 - c
    own = CORES * x + c
    left, right, far = CORES * xl + c, CORES * xr + c, CORES * xo + c
    parts = gath.shape[1]
    half = parts // 2
    rows_y, width = out_ref.shape[0] if not backward else x_ref.shape[0], out_ref.shape[1]
    r = rows_y // chunks
    h = r // 2

    barrier = pltpu.get_barrier_semaphore()
    peers = [me.at(yu, x, c), me.at(yd, x, c), me.at(y, xr, c), me.at(y, xl, c), me.at(y, x, other)]
    if backward:
        peers += [me.at(y, xo, c), me.at(y, xr, other), me.at(y, xl, other), me.at(y, xo, other)]
    for peer in peers:
        pl.semaphore_signal(barrier, inc=1, device_id=peer, device_id_type=pl.DeviceIdType.MESH)

    load = pltpu.make_async_copy(act_hbm, gath.at[own, pl.ds(0, RING)], loc_sem.at[0])
    load.start()
    if backward:
        load_kv = pltpu.make_async_copy(kv_hbm, kvp, loc_sem.at[1])
        load_kv.start()
    wb[pl.ds(0, wt_ref.shape[0]), :] = wt_ref[...].astype(jnp.bfloat16)
    if backward:
        wb[pl.ds(wt_ref.shape[0], wkv_ref.shape[0]), :] = wkv_ref[...]
        load_kv.wait()
    load.wait()
    pl.semaphore_wait(barrier, len(peers))

    def remote(src, dst, send_sem, recv_sem, peer):
        return pltpu.make_async_remote_copy(src_ref=src, dst_ref=dst, send_sem=send_sem, recv_sem=recv_sem,
                                            device_id=peer, device_id_type=pl.DeviceIdType.MESH)

    def block(source, k, first=0, count=parts):
        return gath.at[source, pl.ds(first, count), pl.ds(k * r, r)]

    def gather(event, k, source, peer, first=0, count=parts):
        return remote(block(source, k, first, count), block(source, k, first, count),
                      gs_sem.at[event, k], gr_sem.at[event, k], peer)

    to_right, to_left, to_partner = me.at(y, xr, c), me.at(y, xl, c), me.at(y, x, other)

    def sends(k):
        return [gather(0, k, own, to_right), gather(1, k, own, to_left), gather(2, k, own, to_partner),
                gather(3, k, left, to_right, 0, half), gather(4, k, right, to_left, half, parts - half),
                gather(5, k, left, to_partner), gather(6, k, right, to_partner), gather(7, k, far, to_partner)]

    p_own, p_left, p_right, p_far = [CORES * pos + other for pos in (x, xl, xr, xo)]

    def receives(k):
        return [gather(0, k, left, to_right), gather(1, k, right, to_left), gather(2, k, p_own, to_partner),
                gather(3, k, far, to_right, 0, half), gather(4, k, far, to_left, half, parts - half),
                gather(5, k, p_left, to_partner), gather(6, k, p_right, to_partner), gather(7, k, p_far, to_partner)]

    def rows_of(way, k):
        return pl.ds(k * r + way * h, h)

    def sum_copy(way, step, k):
        d = turn(y, -(1 + step) if way == 0 else 1 + step)
        return remote(part.at[d, rows_of(way, k)], ring.at[way, step, k], rs_sem.at[way, step, k],
                      rr_sem.at[way, step, k], me.at(yu if way == 0 else yd, x, c))

    def multiply(d, k):
        rows = pl.ds(k * r, r)
        pieces = [gath[j, d, rows, :] for j in range(ROW_DEVICES)]
        if backward:
            j = CORES * lax.rem(d, 2) + d // 2
            pieces += [gath[j, RING, rows, :], gath[j, RING + 1, rows, :],
                       gath[j + RING, RING, rows, :], gath[j + RING, RING + 1, rows, :]]
        lhs = jnp.concatenate([piece.astype(jnp.bfloat16) for piece in pieces], axis=1)
        part[d, rows, :] = jnp.dot(lhs, wb[...], preferred_element_type=jnp.float32)

    def advance(k, step):
        for way in (0, 1):
            sum_copy(way, step, k).wait_recv()
            d = turn(y, -(2 + step) if way == 0 else 2 + step)
            part[d, rows_of(way, k), :] += ring[way, step, k]
            if step < RING - 2:
                sum_copy(way, step + 1, k).start()
        if step == RING - 2:
            finish(k)

    def finish(k):
        rows = pl.ds(k * r, r)
        total = part[y, rows, :]
        if not backward:
            out_ref[rows, :] = (x_ref[rows, :].astype(jnp.float32) + total).astype(jnp.bfloat16).astype(jnp.float32)
            return
        unit = x_ref[rows, :].astype(jnp.float32) * inv_ref[rows, :]
        row_sum = jnp.sum(total * gain_ref[...] * unit, axis=1, keepdims=True)
        square = jnp.concatenate([jnp.broadcast_to(row_sum, (r, 128)), jnp.zeros((128 - r, 128), jnp.float32)], axis=0)
        rowpart[k] = jnp.transpose(square)[0:8, :]
        gain_row = jnp.sum(total * unit, axis=0, keepdims=True)
        tail = pl.ds(rows_y, 8)
        row_id = lax.broadcasted_iota(jnp.int32, (8, width), 0)
        addend = jnp.where(row_id == 0, jnp.broadcast_to(gain_row, (8, width)), 0.0)
        out_ref[tail, :] = addend if k == 0 else out_ref[tail, :] + addend

    if backward:
        p = lax.rem(x, 2)
        xn = x + 1 - 2 * p
        mine, theirs = CORES * c + p, CORES * c + 1 - p
        core_copy = remote(kvp.at[pl.ds(CORES * other, CORES)], kv_core, ks_sem.at[0], kr_sem.at[0], to_partner)
        core_copy.start()
        core_copy.wait_recv()

        def chip_copy(k):
            return remote(kv_send.at[:, pl.ds(k * r, r)], kv_chip.at[:, pl.ds(k * r, r)], ks_sem.at[1 + k],
                          kr_sem.at[1 + k], me.at(y, xn, c))

        for k in range(chunks):
            rows = pl.ds(k * r, r)
            kv_send[:, rows, :] = kvp[theirs, :, rows, :] + kv_core[1 - p, :, rows, :]
            chip_copy(k).start()

        def settle_kv(k):
            chip_copy(k).wait_recv()
            rows = pl.ds(k * r, r)
            total = kvp[mine, :, rows, :] + kv_core[p, :, rows, :] + kv_chip[:, rows, :]
            gath[own, pl.ds(RING, 2), rows, :] = total.astype(jnp.bfloat16).astype(jnp.float32)

    def begin(k):
        if backward:
            settle_kv(k)
        for copy in sends(k)[:3]:
            copy.start()

    begin(0)
    if chunks > 1:
        begin(1)
    for k in range(chunks + RING - 1):
        if k < chunks:
            out_going, incoming = sends(k), receives(k)
            incoming[0].wait_recv()
            out_going[3].start()
            out_going[5].start()
            incoming[1].wait_recv()
            out_going[4].start()
            out_going[6].start()
            if k + 2 < chunks:
                begin(k + 2)
        for step in range(RING - 1):
            if 0 <= k - 1 - step < chunks:
                advance(k - 1 - step, step)
        if k < chunks:
            incoming[3].wait_recv()
            incoming[4].wait_recv()
            out_going[7].start()
            for event in (2, 5, 6, 7):
                incoming[event].wait_recv()
            multiply(yd, k)
            sum_copy(0, 0, k).start()
            multiply(yu, k)
            sum_copy(1, 0, k).start()
            multiply(turn(y, 2), k)
            multiply(y, k)

    if backward:
        members = [(pos, core) for pos in (xr, xl, xo) for core in (c, other)] + [(x, other)]

        def mean_copy(n, m):
            pos, core = members[n]
            return remote(rowpart, rowall.at[m], ms_sem.at[n], mr_sem.at[m], me.at(y, pos, core))

        slots = [2, 3, 0, 1, 4, 5, 6]
        copies = [mean_copy(n, slots[n]) for n in range(7)]
        for copy in copies:
            copy.start()
        kv_head = x // 2
        kv_copies = [pltpu.make_async_copy(gath.at[CORES * (2 * kv_head + d % 2) + d // 2, pl.ds(RING, 2)], kv_out.at[d],
                                           loc_sem.at[d]) for d in range(RING)]
        for copy in kv_copies:
            copy.start()
        for copy in copies:
            copy.wait_recv()
        sums = rowpart[...]
        for m in range(7):
            sums = sums + rowall[m]
        d_model = width * ROW_DEVICES
        for k in range(chunks):
            rows = pl.ds(k * r, r)
            mean = jnp.transpose(sums[k])[0:r, 0:1] * (1.0 / d_model)
            inv = inv_ref[rows, :]
            unit = x_ref[rows, :].astype(jnp.float32) * inv
            delta = inv * (part[y, rows, :] * gain_ref[...] - unit * mean)
            out_ref[rows, :] = (dout_ref[rows, :].astype(jnp.float32) + delta).astype(jnp.bfloat16).astype(jnp.float32)
        for copy in kv_copies:
            copy.wait()
        for copy in copies:
            copy.wait_send()
        core_copy.wait_send()
        for k in range(chunks):
            chip_copy(k).wait_send()
    for k in range(chunks):
        for copy in sends(k):
            copy.wait_send()
        for way in (0, 1):
            for step in range(RING - 1):
                sum_copy(way, step, k).wait_send()


def exchange(act, weights, x_block, extra=None, collective_id=0):
    backward = extra is not None
    rows_y, width = x_block.shape
    chunks = CHUNKS
    h = rows_y // chunks // 2
    parts = RING + (2 if backward else 0)
    any_spec = pl.BlockSpec(memory_space=pl.ANY)
    vmem_spec = pl.BlockSpec(memory_space=pltpu.VMEM)
    depth = weights.shape[0] + (extra[1].shape[0] if backward else 0)
    dma = pltpu.SemaphoreType.DMA
    scratch = [
        pltpu.VMEM((ROW_DEVICES, parts, rows_y, HEAD_DIM), jnp.float32),
        pltpu.VMEM((depth, width), jnp.bfloat16),
        pltpu.VMEM((RING, rows_y, width), jnp.float32),
        pltpu.VMEM((2, RING - 1, chunks, h, width), jnp.float32),
    ]
    sems = [dma((8, chunks)), dma((8, chunks)), dma((2, RING - 1, chunks)), dma((2, RING - 1, chunks))]
    if backward:
        kv, w_kv, dout_block, inv_block, gain_block = extra
        args = (act, kv, weights, w_kv, x_block, dout_block, inv_block, gain_block)
        in_specs = [any_spec, any_spec] + [vmem_spec] * 6
        out_shape = (jax.ShapeDtypeStruct((rows_y + 8, width), jnp.float32),
                     jax.ShapeDtypeStruct((RING, 2, rows_y, HEAD_DIM), jnp.float32))
        out_specs = (vmem_spec, any_spec)
        scratch += [
            pltpu.VMEM((RING, 2, rows_y, HEAD_DIM), jnp.float32),
            pltpu.VMEM((CORES, 2, rows_y, HEAD_DIM), jnp.float32),
            pltpu.VMEM((2, rows_y, HEAD_DIM), jnp.float32),
            pltpu.VMEM((2, rows_y, HEAD_DIM), jnp.float32),
            pltpu.VMEM((chunks, 8, 128), jnp.float32),
            pltpu.VMEM((ROW_DEVICES - 1, chunks, 8, 128), jnp.float32),
        ]
        sems += [dma((1 + chunks,)), dma((1 + chunks,)), dma((ROW_DEVICES - 1,)), dma((ROW_DEVICES - 1,))]
    else:
        args = (act, weights, x_block)
        in_specs = [any_spec] + [vmem_spec] * 2
        out_shape = jax.ShapeDtypeStruct((rows_y, width), jnp.float32)
        out_specs = vmem_spec
    sems += [dma((RING,))]
    flops = 2 * RING * rows_y * depth * width
    return pl.pallas_call(
        functools.partial(exchange_kernel, backward, chunks),
        out_shape=out_shape, in_specs=in_specs, out_specs=out_specs, scratch_shapes=scratch + sems,
        compiler_params=pltpu.CompilerParams(collective_id=collective_id, has_side_effects=True, vmem_limit_bytes=VMEM_BYTES),
        cost_estimate=pl.CostEstimate(flops=flops, bytes_accessed=4 * RING * rows_y * width, transcendentals=0),
        name='exchange_bwd' if backward else 'exchange_fwd',
    )(*args)


def narrow(gathered, pad, d_model):
    rows_y, width = gathered.shape[0] // (RING * ROW_DEVICES) - pad, gathered.shape[1]

    def kernel(in_ref, out_ref):
        out_ref[...] = in_ref[pl.ds(0, rows_y), :].astype(jnp.bfloat16)

    return pl.pallas_call(
        kernel, grid=(RING, ROW_DEVICES),
        in_specs=[pl.BlockSpec((rows_y + pad, width), lambda y, i: (y * ROW_DEVICES + i, 0))],
        out_specs=pl.BlockSpec((rows_y, width), lambda y, i: (y, i)),
        out_shape=jax.ShapeDtypeStruct((RING * rows_y, d_model), jnp.bfloat16),
        compiler_params=pltpu.CompilerParams(vmem_limit_bytes=16 * 1024 * 1024),
        cost_estimate=pl.CostEstimate(flops=RING * rows_y * d_model, bytes_accessed=6 * RING * rows_y * d_model, transcendentals=0),
        name='narrow',
    )(gathered)


def solution(mesh):
    tp_size = mesh.shape['tp']
    row_groups = [list(range(first, first + ROW_DEVICES)) for first in range(0, tp_size, ROW_DEVICES)]

    def block_fn(hidden, grad_out, norm_gain, w_query, w_key, w_value, w_out):
        batch, seq_len, d_model = hidden.shape
        kv_heads = w_key.shape[1] // HEAD_DIM
        group_size = tp_size // kv_heads
        index = lax.axis_index('tp')
        y, column = index // ROW_DEVICES, index % ROW_DEVICES
        tokens, width = batch * seq_len, d_model // ROW_DEVICES
        rows_y = tokens // RING
        kv_pair = ROW_DEVICES // group_size * HEAD_DIM

        def spread(weight):
            blocks = weight.astype(jnp.float32).reshape(HEAD_DIM, ROW_DEVICES, width).transpose(1, 0, 2)
            got = lax.all_to_all(blocks, 'tp', 0, 0, axis_index_groups=row_groups, tiled=True)
            return got.reshape(ROW_DEVICES * HEAD_DIM, width)

        def own_block(array):
            return lax.dynamic_slice(array.reshape(tokens, d_model), (y * rows_y, column * width), (rows_y, width))

        def kv_block(weight):
            block = lax.dynamic_slice(weight, (column * width, y * kv_pair), (width, kv_pair))
            return block.T.reshape(-1, 1, HEAD_DIM, width)

        w_out_block = spread(w_out)
        w_query_block = spread(w_query.T)
        w_kv_block = jnp.concatenate([kv_block(w_key), kv_block(w_value)], axis=1).reshape(-1, width)

        kv_index = index // group_size
        w_kv = jnp.concatenate([
            lax.dynamic_slice_in_dim(w_key, kv_index * HEAD_DIM, HEAD_DIM, axis=1),
            lax.dynamic_slice_in_dim(w_value, kv_index * HEAD_DIM, HEAD_DIM, axis=1)], axis=1)
        cos_t, sin_t = rope_tables(seq_len)

        hidden_f32 = hidden.astype(jnp.float32)
        inv_rms = lax.rsqrt(jnp.mean(hidden_f32 * hidden_f32, axis=-1, keepdims=True) + NORM_EPS)
        gain_f32 = norm_gain.astype(jnp.float32)
        normed = (hidden_f32 * inv_rms * gain_f32).astype(jnp.bfloat16)
        q_proj = jnp.einsum('bsd,de->bse', normed, w_query, preferred_element_type=jnp.float32)
        q_rot = rotate_pairs(q_proj[:, :, None, :], cos_t, sin_t).astype(jnp.bfloat16)
        kv_proj = jnp.einsum('bsd,de->bse', normed, w_kv, preferred_element_type=jnp.float32)
        k_rot = rotate_pairs(kv_proj[:, :, None, :HEAD_DIM], cos_t, sin_t)[:, :, 0, :].astype(jnp.bfloat16)
        v_head = kv_proj[:, :, HEAD_DIM:].astype(jnp.bfloat16)
        scores = jnp.einsum('bqjh,bkh->bjqk', q_rot, k_rot, preferred_element_type=jnp.float32) * SCORE_SCALE
        causal = jnp.arange(seq_len)[:, None] >= jnp.arange(seq_len)[None, :]
        attn_probs = jax.nn.softmax(jnp.where(causal, scores, MASK_VALUE), axis=-1)
        probs_bf16 = attn_probs.astype(jnp.bfloat16)
        attn_heads = jnp.einsum('bjqk,bkh->bqjh', probs_bf16, v_head, preferred_element_type=jnp.float32).astype(jnp.bfloat16)
        attn_flat = attn_heads.reshape(batch, seq_len, HEAD_DIM)
        attn_send = lax.optimization_barrier(attn_flat).astype(jnp.float32).reshape(RING, rows_y, HEAD_DIM)
        x_block = own_block(hidden)
        out_block = exchange(attn_send, w_out_block, x_block, collective_id=1)
        out_all = lax.all_gather(out_block, 'tp', axis=0, tiled=True)
        block_out = narrow(out_all, 0, d_model).reshape(batch, seq_len, d_model)

        grad_w_out = jnp.einsum('bse,bsd->ed', attn_flat, grad_out, preferred_element_type=jnp.float32)
        grad_heads = jnp.einsum('bsd,ed->bse', grad_out, w_out, preferred_element_type=jnp.float32).astype(jnp.bfloat16)[:, :, None, :]
        grad_probs = jnp.einsum('bqjh,bkh->bjqk', grad_heads, v_head, preferred_element_type=jnp.float32)
        grad_v = jnp.einsum('bjqk,bqjh->bkh', probs_bf16, grad_heads, preferred_element_type=jnp.float32)
        row_dot = jnp.sum(attn_probs * grad_probs, axis=-1, keepdims=True)
        grad_scores = (attn_probs * (grad_probs - row_dot) * SCORE_SCALE).astype(jnp.bfloat16)
        grad_q_rot = jnp.einsum('bjqk,bkh->bqjh', grad_scores, k_rot, preferred_element_type=jnp.float32)
        grad_k_rot = jnp.einsum('bjqk,bqjh->bkh', grad_scores, q_rot, preferred_element_type=jnp.float32)
        grad_q = rotate_pairs(grad_q_rot, cos_t, -sin_t).astype(jnp.bfloat16).reshape(batch, seq_len, HEAD_DIM)
        grad_k = rotate_pairs(grad_k_rot[:, :, None, :], cos_t, -sin_t)[:, :, 0, :]
        grad_q_send = lax.optimization_barrier(grad_q).astype(jnp.float32).reshape(RING, rows_y, HEAD_DIM)
        grad_kv_send = jnp.stack([grad_k.reshape(RING, rows_y, HEAD_DIM), grad_v.reshape(RING, rows_y, HEAD_DIM)], axis=1)
        inv_block = lax.dynamic_slice(inv_rms.reshape(tokens, 1), (y * rows_y, 0), (rows_y, 1))
        gain_block = lax.dynamic_slice(gain_f32.reshape(1, d_model), (0, column * width), (1, width))
        grad_block, grad_kv = exchange(grad_q_send, w_query_block, x_block,
                                       (grad_kv_send, w_kv_block, own_block(grad_out), inv_block, gain_block), collective_id=2)
        grad_all = lax.all_gather(grad_block, 'tp', axis=0, tiled=True)
        grad_hidden = narrow(grad_all, 8, d_model).reshape(batch, seq_len, d_model)
        gain_rows = grad_all.reshape(RING, ROW_DEVICES, rows_y + 8, width)[:, :, rows_y, :]
        grad_gain = jnp.sum(gain_rows, axis=0).reshape(d_model)

        grad_w_query = jnp.einsum('bsd,bse->de', normed, grad_q, preferred_element_type=jnp.float32)
        normed_flat = normed.reshape(tokens, d_model)
        grad_kv = grad_kv.astype(jnp.bfloat16)
        grad_w_key = jnp.einsum('sd,se->de', normed_flat, grad_kv[:, 0].reshape(tokens, HEAD_DIM), preferred_element_type=jnp.float32)
        grad_w_value = jnp.einsum('sd,se->de', normed_flat, grad_kv[:, 1].reshape(tokens, HEAD_DIM), preferred_element_type=jnp.float32)
        return block_out, grad_hidden, grad_gain, grad_w_query, grad_w_key, grad_w_value, grad_w_out

    act_spec = P('dp', None, None)
    return jax.shard_map(
        block_fn, mesh=mesh,
        in_specs=(act_spec, act_spec, P(None), P(None, 'tp'), P(None, None), P(None, None), P('tp', None)),
        out_specs=(act_spec, act_spec, P('dp'), P('dp', 'tp'), P('dp', 'tp'), P('dp', 'tp'), P(('dp', 'tp'), None)),
        check_vma=False)
```

time: 1000 us -> 621 us (0.62)
  waiting for transfers between devices: 652 us -> 74.1 us
  Pallas kernels: 0 us -> 330 us
  other arithmetic: 135 us -> 53 us
  matrix products: 162 us -> 91.4 us
  starting transfers between devices: 3.27 us -> 14.6 us
    psum x1 -> x0, waiting for transfers between devices: 498 us -> none  [block_fn(): attn_sum = lax.psum(out_part, 'tp')]
    pallas_call x0 -> x4, Pallas kernels: none -> 330 us  [the longest x2 262 us: exchange(): pl.pallas_call(functools.partial(exchange_kernel, backward, chunks), out_...]
    ppermute x2 -> x0, waiting for transfers between devices: 154 us -> none  [group_sum(): total = total + lax.ppermute(total, 'tp', perm=partner_pairs)]
    all_gather x0 -> x2, waiting for transfers between devices: none -> 66.7 us  [the longest x1 66.7 us: block_fn(): grad_all = lax.all_gather(grad_block, 'tp', axis=0, tiled=True)]
    dot_general x4 -> x2, matrix products: 82 us -> 16.3 us  [the longest x1 8.16 us: block_fn(): jnp.einsum('sd,se->de', normed_flat, grad_kv[:, 0].reshape(tokens, HEAD_D...]
    convert_element_type x1 -> x2, other arithmetic: 60.7 us -> 23.8 us  [the longest x1 21.9 us: block_fn(): normed = (hidden_f32 * inv_rms * gain_f32).astype(jnp.bfloat16)]
    reduce_sum x1, other arithmetic: 26.4 us -> 1.16 us  [block_fn(): grad_gain = jnp.sum(gain_rows, axis=0).reshape(d_model)]
    another operation x3, other arithmetic: 24 us -> 5.16 us
  transfers between devices with their start and end apart: 3 -> 4, of which waited for: 3 -> 2; matrix products, arithmetic and copies ran while one was open for 4% -> 28% of each run, Pallas kernels for 0% -> 35%
where the time goes in v2:
time: 621 us; the launch traced here: 612 us
  Pallas kernels  330 us (53%)
  matrix products  91.4 us (15%)
  waiting for transfers between devices  74.1 us (12%)
  other arithmetic  53 us (9%)
  local copies, waits for them, and re-layouts  33.3 us (5%)
  between operations  15 us (2%)
  starting transfers between devices  14.6 us (2%)
    pallas_call x2, Pallas kernels, exchange(): pl.pallas_call(functools.partial(exchange_kernel, backward, chunks), out_...  262 us
    pallas_call x2, Pallas kernels, narrow(): pl.pallas_call(kernel, grid=(RING, ROW_DEVICES), in_specs=[pl.BlockSpec((...  68.1 us
    all_gather x1, waiting for transfers between devices, block_fn(): grad_all = lax.all_gather(grad_block, 'tp', axis=0, tiled=True)  66.7 us
    convert_element_type x1, other arithmetic, block_fn(): normed = (hidden_f32 * inv_rms * gain_f32).astype(jnp.bfloat16)  21.9 us
    all_to_all x2, starting transfers between devices, spread(): lax.all_to_all(blocks, 'tp', 0, 0, axis_index_groups=row_groups, tiled=True)  14.6 us
    dot_general x1, matrix products, block_fn(): jnp.einsum('bsd,bse->de', normed, grad_q, preferred_element_type=jnp.floa...  13.4 us
    dot_general x1, matrix products, block_fn(): jnp.einsum('bse,bsd->ed', attn_flat, grad_out, preferred_element_type=jnp...  12.8 us
  transfers between devices with their start and end apart: 4, of which 2 were waited for; matrix products, arithmetic and copies ran while one was open for 28% of the time, Pallas kernels for 35%

profile of v2, /device:TPU:97, one launch (start us, length us, event | category | flops | bytes accessed | tf_op | source)
XLA Modules:
  0.0 611.6 jit_solution(6078212658041557151)
XLA Ops:
  10.4 6.3 %all-to-all-start = ((f32[8,128,640]{2,1,0:T(8,128)}), f32[8,128,640]{2,1,0:T(8,128)}, u32[]{:S(2)}, u32[]{:S(2)}) async-start(f32[8,128,640]{2,1,0:T(8,128)} %bitcast.130), calls=%async_computation | async-start | bytes 5242880 | tf_op jit(solution)/shard_map/all_to_all | solution.py:347
  16.8 10.0 %fusion = f32[3,768]{1,0:T(4,128)S(1)} fusion(bf16[3,768,5120]{2,1,0:T(8,128)(2,1)} %param.7), kind=kLoop, calls=%fused_computation.2 | loop fusion | flops 35387136 | bytes 23602176 | tf_op jit(solution)/shard_map/reduce_sum | solution.py:368
  33.1 21.9 %fusion.2 = bf16[3,768,5120]{2,1,0:T(8,128)(2,1)} fusion(bf16[3,768,5120]{2,1,0:T(8,128)(2,1)} %param.7, f32[5120]{0:T(1024)S(1)} %convert_element_type.58, f32[3,768]{1,0:T(4,128)S(1)} %get-tuple-element.26), kind=kLoop, calls=%fused_computation.4 | loop fusion | flops 47185920 | bytes 47215616 | tf_op jit(solution)/shard_map/convert_element_type | solution.py:370
  55.0 11.2 %fusion.15 = f32[3,768,256]{1,2,0:T(8,128)S(1)} fusion(bf16[3,768,5120]{2,1,0:T(8,128)(2,1)} %fusion.2, bf16[5120,128]{0,1:T(8,128)(2,1)S(1)} %copy-done.10, bf16[5120,128]{0,1:T(8,128)(2,1)S(1)} %copy-done.11), kind=kOutput, calls=%fused_computation.25 | convolution fusion | flops 6045040640 | bytes 28573696 | tf_op jit(solution)/shard_map/bsd,de->bse/dot_general | solution.py:373
  68.5 11.9 %fusion.23 = f32[3,768,128]{1,2,0:T(8,128)S(1)} fusion(bf16[3,768,5120]{2,1,0:T(8,128)(2,1)} %fusion.2, bf16[5120,128]{1,0:T(8,128)(2,1)S(1)} %copy-done.1), kind=kOutput, calls=%fused_computation.36 | convolution fusion | flops 3019898880 | bytes 26083328 | tf_op jit(solution)/shard_map/bsd,de->bse/dot_general | solution.py:371
  88.0 2.8 fusion.25
  92.1 2.0 dynamic_slice.26.refs_2_.refs_4_
  94.1 80.6 %exchange_fwd.1 = f32[576,640]{1,0:T(8,128)} custom-call(f32[4,576,128]{2,1,0:T(8,128)} %bitcast.158, f32[1024,640]{1,0:T(8,128)} %bitcast.12.refs_1_, bf16[576,640]{1,0:T(8,128)(2,1)} %dynamic_slice.26.refs_2_.refs_4_), custom_call_target="tpu_custom_call" | custom-call | flops 3019898880 | bytes 5898240 | tf_op jit(solution)/shard_map/exchange_fwd/pallas_call | solution.py:305
  176.3 2.1 copy.61
  178.3 8.3 %all-to-all-start.1 = ((f32[8,128,640]{2,1,0:T(8,128)}), f32[8,128,640]{2,1,0:T(8,128)}, u32[]{:S(2)}, u32[]{:S(2)}) async-start(f32[8,128,640]{2,1,0:T(8,128)} %bitcast.142), calls=%async_computation.1 | async-start | bytes 5242880 | tf_op jit(solution)/shard_map/all_to_all | solution.py:347
  186.6 12.0 %convolution_convert_fusion = bf16[3,768,128]{2,1,0:T(8,128)(2,1)S(1)} fusion(bf16[3,768,5120]{2,1,0:T(8,128)(2,1)} %param.8, bf16[128,5120]{1,0:T(8,128)(2,1)} %param.13), kind=kOutput, calls=%fused_computation.34 | convolution fusion | flops 3020193792 | bytes 25493504 | tf_op jit(solution)/shard_map/bsd,ed->bse/dot_general | solution.py:389
  198.6 2.8 fusion.3
  201.5 2.8 fusion.10
  212.0 2.1 dynamic_slice.29.refs_5_
  228.2 4.5 fusion.11
  234.3 7.3 %all-to-all-done.1 = f32[8,128,640]{2,1,0:T(8,128)} async-done(((f32[8,128,640]{2,1,0:T(8,128)}), f32[8,128,640]{2,1,0:T(8,128)}, u32[]{:S(2)}, u32[]{:S(2)}) %all-to-all-start.1) | async-done | bytes 2621472 | tf_op jit(solution)/shard_map/all_to_all | solution.py:347
  241.6 181.4 %exchange_bwd.1 = (f32[584,640]{1,0:T(8,128)}, f32[4,2,576,128]{3,2,1,0:T(8,128)}) custom-call(f32[4,576,128]{2,1,0:T(8,128)} %bitcast.157, f32[4,2,576,128]{3,2,1,0:T(8,128)} %pad_maximum_fusion.refs_1_, f32[1024,640]{1,0:T(8,128)} %bitcast.28.refs_2_, bf16[512,640]{1,0:T(8,128)(2,1)} %bitcast.160, bf16[576,640]{1,0:T(8,128)(2,1)} %dynamic_slice.26.refs_2_.refs_4_, ...), custom_call_target="tpu_custom_call" | custom-call | flops 4529848320 | bytes 5898240 | tf_op jit(solution)/shard_map/exchange_bwd/pallas_call | solution.py:305
  423.2 12.8 %convolution_bitcast_fusion = f32[128,5120]{1,0:T(8,128)} fusion(bf16[3,768,128]{1,2,0:T(8,128)(2,1)S(1)} %copy-done.3, bf16[3,768,5120]{2,1,0:T(8,128)(2,1)} %param.8), kind=kOutput, calls=%fused_computation.15 | convolution fusion | flops 3019898880 | bytes 26804224 | tf_op jit(solution)/shard_map/bse,bsd->ed/dot_general | solution.py:388
  436.0 13.4 %convolution_bitcast_fusion.1 = f32[5120,128]{1,0:T(8,128)} fusion(bf16[3,768,5120]{2,1,0:T(8,128)(2,1)} %fusion.2, bf16[3,768,128]{1,2,0:T(8,128)(2,1)S(1)} %copy.83), kind=kOutput, calls=%fused_computation.16 | convolution fusion | flops 3019898880 | bytes 26804224 | tf_op jit(solution)/shard_map/bsd,bse->de/dot_general | solution.py:409
  451.5 8.2 %fusion.43 = f32[5120,128]{1,0:T(8,128)} fusion(bf16[2304,5120]{1,0:T(8,128)(2,1)S(1)} %bitcast.134, bf16[2304,128]{1,0:T(8,128)(2,1)S(1)} %bitcast.162), kind=kOutput, calls=%fused_computation.74 | convolution fusion | flops 3019898880 | bytes 26804224 | tf_op jit(solution)/shard_map/sd,se->de/dot_general | solution.py:412
  459.6 8.2 %fusion.44 = f32[5120,128]{1,0:T(8,128)} fusion(bf16[2304,5120]{1,0:T(8,128)(2,1)S(1)} %bitcast.135, bf16[2304,128]{1,0:T(8,128)(2,1)S(1)} %bitcast.161), kind=kOutput, calls=%fused_computation.75 | convolution fusion | flops 3019898880 | bytes 26804224 | tf_op jit(solution)/shard_map/sd,se->de/dot_general | solution.py:413
  467.8 34.0 %narrow.2 = bf16[2304,5120]{1,0:T(8,128)(2,1)} custom-call(f32[18432,640]{1,0:T(8,128)} %all-gather.3.cloned.1.call-done.in_ref), custom_call_target="tpu_custom_call" | custom-call | flops 11796480 | bytes 70778880 | tf_op jit(solution)/shard_map/narrow/pallas_call | solution.py:320
  501.8 66.7 %all-gather.5.cloned.1.call-done.in_ref = f32[18688,640]{1,0:T(8,128)} async-done(((f32[584,640]{1,0:T(8,128)}), f32[18688,640]{1,0:T(8,128)}) %all-gather.5.cloned.1.call-update) | async-done | bytes 47841296 | tf_op jit(solution)/shard_map/all_gather | solution.py:404
  570.2 34.1 %narrow.3 = bf16[2304,5120]{1,0:T(8,128)(2,1)} custom-call(f32[18688,640]{1,0:T(8,128)} %all-gather.5.cloned.1.call-done.in_ref), custom_call_target="tpu_custom_call" | custom-call | flops 11796480 | bytes 70778880 | tf_op jit(solution)/shard_map/narrow/pallas_call | solution.py:320
  (105 shorter events, 49.3 us)
Async XLA Ops:
  10.4 83.7 %all-to-all-start = ((f32[8,128,640]{2,1,0:T(8,128)}), f32[8,128,640]{2,1,0:T(8,128)}, u32[]{:S(2)}, u32[]{:S(2)}) async-start(f32[8,128,640]{2,1,0:T(8,128)} %bitcast.130), calls=%async_computation | async-start | bytes 5242880 | tf_op jit(solution)/shard_map/all_to_all | solution.py:347
  16.7 451.1 %all-gather.3.cloned.1.call-start = ((), (), s32[]{:S(2)}) async-start(), calls=%async_computation.2 | async-start | bytes 48660480 | tf_op jit(solution)/shard_map/all_gather | solution.py:385
  16.8 10.0 %copy-start.16 = (bf16[5120]{0:T(1024)(128)(2,1)S(1)}, bf16[5120]{0:T(1024)(128)(2,1)}, u32[]{:S(2)}) copy-start(bf16[5120]{0:T(1024)(128)(2,1)} %param.9) | copy-start | bytes 30724
  28.2 53.0 %copy-start.8 = (f32[768,64]{0,1:T(8,128)}, f32[768,64]{0,1:T(8,128)S(1)}, u32[]{:S(2)}) copy-start(f32[768,64]{0,1:T(8,128)S(1)} %get-tuple-element.29) | copy-start | bytes 589828
  33.1 21.9 %copy-start.10 = (bf16[5120,128]{0,1:T(8,128)(2,1)S(1)}, bf16[5120,128]{0,1:T(8,128)(2,1)}, u32[]{:S(2)}) copy-start(bf16[5120,128]{0,1:T(8,128)(2,1)} %copy.93) | copy-start | bytes 3932164
  33.1 21.9 %copy-start.11 = (bf16[5120,128]{0,1:T(8,128)(2,1)S(1)}, bf16[5120,128]{0,1:T(8,128)(2,1)}, u32[]{:S(2)}) copy-start(bf16[5120,128]{0,1:T(8,128)(2,1)} %copy.92) | copy-start | bytes 3932164
  55.0 13.5 %copy-start.1 = (bf16[5120,128]{1,0:T(8,128)(2,1)S(1)}, bf16[5120,128]{1,0:T(8,128)(2,1)}, u32[]{:S(2)}) copy-start(bf16[5120,128]{1,0:T(8,128)(2,1)} %param.10) | copy-start | bytes 3932164
  83.1 3.5 copy-start.6
  83.3 4.7 copy-start.14
  90.8 83.9 %copy-start.2 = (bf16[3,768,128]{1,2,0:T(8,128)(2,1)}, bf16[3,768,128]{1,2,0:T(8,128)(2,1)S(1)}, u32[]{:S(2)}) copy-start(bf16[3,768,128]{1,2,0:T(8,128)(2,1)S(1)} %fusion.25) | copy-start | bytes 1769476
  178.3 20.3 %slice-start.6 = ((s8[7077888]{0:T(1024)(128)(4,1)}), s8[2883584]{0:T(1024)(128)(4,1)S(1)}, s32[]{:S(2)}) async-start(s8[7077888]{0:T(1024)(128)(4,1)} %bitcast.138), calls=%async_computation.10 | async-start | bytes 5767168
  178.3 63.3 %all-to-all-start.1 = ((f32[8,128,640]{2,1,0:T(8,128)}), f32[8,128,640]{2,1,0:T(8,128)}, u32[]{:S(2)}, u32[]{:S(2)}) async-start(f32[8,128,640]{2,1,0:T(8,128)} %bitcast.142), calls=%async_computation.1 | async-start | bytes 5242880 | tf_op jit(solution)/shard_map/all_to_all | solution.py:347
  186.6 381.9 %all-gather.5.cloned.1.call-start = ((), (), s32[]{:S(2)}) async-start(), calls=%async_computation.3 | async-start | bytes 49336320 | tf_op jit(solution)/shard_map/all_gather | solution.py:404
  186.6 12.0 %slice-start.7 = ((s8[7077888]{0:T(1024)(128)(4,1)}), s8[4194304]{0:T(1024)(128)(4,1)S(1)}, s32[]{:S(2)}) async-start(s8[7077888]{0:T(1024)(128)(4,1)} %bitcast.138), calls=%async_computation.11 | async-start | bytes 8388608
  186.6 12.0 %copy-start.15 = (f32[3,768,256]{1,2,0:T(8,128)S(1)}, f32[3,768,256]{1,2,0:T(8,128)}, u32[]{:S(2)}) copy-start(f32[3,768,256]{1,2,0:T(8,128)} %copy-done.13) | copy-start | bytes 7077892
  205.4 11.8 %copy-start.9 = (f32[768,64]{0,1:T(8,128)S(1)}, f32[768,64]{0,1:T(8,128)}, u32[]{:S(2)}) copy-start(f32[768,64]{0,1:T(8,128)} %copy-done.8) | copy-start | bytes 589828
  212.0 5.2 copy-start.12
  241.6 181.5 %copy-start.3 = (bf16[3,768,128]{1,2,0:T(8,128)(2,1)S(1)}, bf16[3,768,128]{1,2,0:T(8,128)(2,1)}, u32[]{:S(2)}) copy-start(bf16[3,768,128]{1,2,0:T(8,128)(2,1)} %copy-done.2) | copy-start | bytes 1769476
  423.2 28.3 %slice-start = ((s8[23592960]{0:T(1024)(128)(4,1)}), s8[4194304]{0:T(1024)(128)(4,1)S(1)}, s32[]{:S(2)}) async-start(s8[23592960]{0:T(1024)(128)(4,1)} %bitcast.132), calls=%async_computation.4 | async-start | bytes 8388608
  423.2 28.3 %slice-start.1 = ((s8[23592960]{0:T(1024)(128)(4,1)}), s8[4194304]{0:T(1024)(128)(4,1)S(1)}, s32[]{:S(2)}) async-start(s8[23592960]{0:T(1024)(128)(4,1)} %bitcast.132), calls=%async_computation.5 | async-start | bytes 8388608
  423.2 28.2 %slice-start.2 = ((s8[23592960]{0:T(1024)(128)(4,1)}), s8[4194304]{0:T(1024)(128)(4,1)S(1)}, s32[]{:S(2)}) async-start(s8[23592960]{0:T(1024)(128)(4,1)} %bitcast.132), calls=%async_computation.6 | async-start | bytes 8388608
  423.2 28.2 %slice-start.3 = ((s8[23592960]{0:T(1024)(128)(4,1)}), s8[2621440]{0:T(1024)(128)(4,1)S(1)}, s32[]{:S(2)}) async-start(s8[23592960]{0:T(1024)(128)(4,1)} %bitcast.132), calls=%async_computation.7 | async-start | bytes 5242880
  436.0 15.4 %slice-start.4 = ((s8[23592960]{0:T(1024)(128)(4,1)}), s8[4194304]{0:T(1024)(128)(4,1)S(1)}, s32[]{:S(2)}) async-start(s8[23592960]{0:T(1024)(128)(4,1)} %bitcast.132), calls=%async_computation.8 | async-start | bytes 8388608
  436.0 15.4 %slice-start.5 = ((s8[23592960]{0:T(1024)(128)(4,1)}), s8[4194304]{0:T(1024)(128)(4,1)S(1)}, s32[]{:S(2)}) async-start(s8[23592960]{0:T(1024)(128)(4,1)} %bitcast.132), calls=%async_computation.9 | async-start | bytes 8388608
  (6 other events, 13.6 us)
Sparse Core Ops, SparseCore 0:
  174.9 238.9 all-gather.2
  423.3 145.1 all-gather.4
